TPU v7x, 256 devices: a whole 4x4x8 slice. The times are simulated.
256 devices in a mesh: seg: 4 (over z_hi), ch: 64 (over x, y, z_lo, core).
Axes of the slice: x: 4, y: 4, z: 8 (z_hi: 4, z_lo: 2; z = z_hi * 2 + z_lo), core: 2. Of those that a mesh axis runs over, the one named last changes fastest.
Arguments:
- gate_in: bfloat16 [1536, 16384], P('ch', 'seg'), may hold values from -6 to 6
- key_in: bfloat16 [1536, 16384], P('ch', 'seg'), may hold values from -6 to 6
- value_in: bfloat16 [1536, 16384], P('ch', 'seg'), may hold values from -6 to 6
- kernel: float32 [1536, 16384], P('ch'), may hold values from -0.046875 to 0.046875
- skip_gain: float32 [1536], P('ch'), may hold values from -1 to 1
- out_weight: bfloat16 [1536, 1536], P('ch'), may hold values from -0.15625 to 0.15625
Outputs:
- output: bfloat16 [16384, 1536], P(('seg', 'ch'))
All inputs are finite; a program needn't handle non-finite values.
Results may differ from a plain program's by a relative error of at most 0.0095.
Values may be sent and summed in bfloat16 or wider, within the bound.
A program may use at most 64 MiB of HBM per device.

v0:
```python
import math

import jax
import jax.numpy as jnp
import numpy as np
from jax import lax
from jax.experimental import pallas as pl
from jax.experimental.pallas import tpu as pltpu
from jax.sharding import PartitionSpec as P

MESH = pl.DeviceIdType.MESH
f32, bf16 = jnp.float32, jnp.bfloat16

SEGS = 4
NX, NY, NZ, CORES = 4, 4, 2, 2
CHIPS = NX * NY * NZ
L = 128
D = 1536
HERE = 24
OWN = HERE // SEGS
LOCAL = 4096
T = SEGS * LOCAL
TILES = LOCAL // L
PITCH = TILES + 8
KPITCH = T // L + 8
WIN = 16
CHUNKS = 4
COLS = D // CHUNKS
HALF = D // 2
PAIRS = OWN // 2
FAR_FIRST = (2, 1, 3)


def halves(table):
    high = table.astype(jnp.bfloat16)
    low = (table - high.astype(np.float32)).astype(jnp.bfloat16)
    return high, low


def tables():
    i = np.arange(L)
    outer = np.exp(-2j * np.pi * np.outer(i + 0.25, i) / L)
    twist = np.exp(-2j * np.pi * np.outer(i + 0.25, i) / T)
    inner = np.exp(-2j * np.pi * np.outer(i, i) / L)
    a2 = np.concatenate([outer.real, outer.imag], 0).astype(np.float32)
    d2 = np.block([[inner.real, inner.imag], [-inner.imag, inner.real]]).astype(np.float32)
    di = np.block([[inner.real, -inner.imag], [inner.imag, inner.real]]).astype(np.float32)
    a_high, a_low = halves(a2)
    d_high, d_low = halves(d2)
    back = (a2.T / T).astype(jnp.bfloat16)
    wide = np.concatenate([d_high, d_low, di.astype(jnp.bfloat16), back], 0)
    narrow = np.concatenate([a_high, a_low], 0)
    twiddle = np.concatenate([twist.real, twist.imag], 0).astype(np.float32)
    return wide, narrow, twiddle


def dot(a, b):
    return jnp.dot(a, b, preferred_element_type=f32)


def split(x):
    high = x.astype(bf16)
    return high, (x - high.astype(f32)).astype(bf16)


def kernel(
    gate_h, key_h, value_h, filt_h, skip_h, weight_h, wide_h, narrow_h, twiddle_h,
    out_ref,
    gate_v, key_v, value_v, filt_v, wide, narrow, twiddle,
    skip_s, strip, mixed_b, x_in, filt_x, spectrum, conv_out, conv_in, skip_v,
    outgoing, gathered, w_all, partial, partner,
    load_sem, x_send, x_recv, b_send, b_recv, w1_send, w1_recv,
    w2_send, w2_recv, w3_send, w3_recv, w4_send, w4_recv, w5_send, w5_recv,
    g_send, g_recv, p_send, p_recv,
):
    seg = lax.axis_index("seg")
    ch = lax.axis_index("ch")
    core = lax.rem(ch, CORES)
    chip = lax.div(ch, CORES)
    cx, cy, cz = lax.div(chip, NY * NZ), lax.rem(lax.div(chip, NZ), NY), lax.rem(chip, NZ)

    def at_seg(step):
        return lax.rem(seg + step, SEGS)

    def at_chip(other):
        return (seg, other * CORES + core)

    barrier = pltpu.get_barrier_semaphore()
    for step in range(1, SEGS):
        pl.semaphore_signal(barrier, inc=1, device_id=(at_seg(step), ch), device_id_type=MESH)
    other_core = (seg, chip * CORES + 1 - core)
    beside = chip + 1 - 2 * cz
    across = (lax.rem(seg + SEGS - 1 + 2 * cz, SEGS), beside * CORES + core)
    for device in (other_core, across):
        pl.semaphore_signal(barrier, inc=1, device_id=device, device_id_type=MESH)

    def greet(step, carry):
        pl.semaphore_signal(
            barrier, inc=1, device_id=at_chip(lax.rem(chip + step, CHIPS)), device_id_type=MESH
        )
        return carry

    lax.fori_loop(1, CHIPS, greet, 0)

    window = pl.multiple_of(lax.div(seg, 2) * 8, 8)
    loads = [
        pltpu.make_async_copy(src, dst, load_sem.at[n])
        for n, (src, dst) in enumerate(
            (
                (key_h, key_v),
                (value_h, value_v),
                (weight_h, w_all.at[0, 0, 0]),
                (filt_h.at[pl.ds(window, WIN), :], filt_v),
                (narrow_h, narrow),
                (twiddle_h, twiddle),
                (wide_h, wide),
                (gate_h, gate_v),
                (skip_h, skip_s),
            )
        )
    ]
    for load in loads:
        load.start()

    def rcopy(src, dst, send, recv, device):
        return pltpu.make_async_remote_copy(
            src_ref=src, dst_ref=dst, send_sem=send, recv_sem=recv, device_id=device, device_id_type=MESH
        )

    loads[0].wait()
    loads[1].wait()

    def mix(j, carry):
        cols = pl.ds(pl.multiple_of(j * L, L), L)
        product = key_v[:, cols].astype(f32) * value_v[:, cols].astype(f32)
        strip[pl.ds(j, HERE, stride=PITCH), :] = product
        return carry

    lax.fori_loop(0, TILES, mix, 0, unroll=4)
    for c in range(HERE):
        mixed_b[c] = strip[c * PITCH : c * PITCH + TILES, :].astype(bf16)

    pl.semaphore_wait(barrier, SEGS - 1 + 2 + CHIPS - 1)

    seg_rows = pl.ds(pl.multiple_of(seg * TILES, TILES), TILES)

    def x_copy(p, step):
        return rcopy(
            mixed_b.at[pl.ds(at_seg(step) * OWN + 2 * p, 2)],
            x_in.at[pl.ds(2 * p, 2), seg_rows, :],
            x_send.at[3 * p + step - 1],
            x_recv.at[3 * p + step - 1],
            (at_seg(step), ch),
        )

    left, right = pl.ds(0, HALF), pl.ds(HALF, HALF)
    z_copies = [
        rcopy(w_all.at[0, 0, 0, :, cols], w_all.at[1, 0, 0, :, cols], w1_send.at[n], w1_recv.at[n], device)
        for n, (cols, device) in enumerate(((left, at_chip(beside)), (right, across)))
    ]

    def x_peer(step):
        return at_chip((lax.rem(cx + step, NX) * NY + cy) * NZ + cz)

    def y_peer(step):
        return at_chip((cx * NY + lax.rem(cy + step, NY)) * NZ + cz)

    def first_copies(z, send, recv):
        own = w_all.at[z, 0, 0]
        return [
            rcopy(own, w_all.at[z, 0, NX - step], send.at[step - 1], recv.at[step - 1], x_peer(step))
            for step in range(1, NX)
        ] + [
            rcopy(own, w_all.at[z, NY - step, 0], send.at[step + 2], recv.at[step + 2], y_peer(step))
            for step in range(1, NY)
        ]

    def second_copies(z, send, recv):
        along_x, along_y = w_all.at[z, 0, 1:, :, left], w_all.at[z, 1:, 0, :, right]
        return [
            rcopy(along_x, w_all.at[z, NY - step, 1:, :, left], send.at[step - 1], recv.at[step - 1], y_peer(step))
            for step in range(1, NY)
        ] + [
            rcopy(along_y, w_all.at[z, 1:, NX - step, :, right], send.at[step + 2], recv.at[step + 2], x_peer(step))
            for step in range(1, NX)
        ]

    loads[2].wait()
    w_a = first_copies(0, w2_send, w2_recv)
    for p in range(PAIRS):
        for step in FAR_FIRST:
            x_copy(p, step).start()
        if p == 0:
            for copy in z_copies + w_a:
                copy.start()
    x_in[:, seg_rows, :] = mixed_b[pl.ds(seg * OWN, OWN)]

    loads[3].wait()
    for n in (4, 5, 6):
        loads[n].wait()

    def turn(j, carry):
        filt_x[pl.ds(j, WIN, stride=KPITCH), :] = filt_v[:, pl.ds(pl.multiple_of(j * L, L), L)]
        return carry

    lax.fori_loop(0, T // L, turn, 0, unroll=4)

    first = seg * OWN - window
    b_re, b_im = twiddle.at[:L, :], twiddle.at[L:, :]

    def spread(u, n):
        u_re, u_im = u[:L, n * L : (n + 1) * L], u[L:, n * L : (n + 1) * L]
        re, im = b_re[...], b_im[...]
        return jnp.concatenate([u_re * re - u_im * im, u_re * im + u_im * re], axis=1)

    def filter_spectrum(p, carry):
        strips = [
            filt_x[pl.ds(pl.multiple_of((first + 2 * p + n) * KPITCH, 8), T // L), :] for n in range(2)
        ]
        high, low = split(jnp.concatenate(strips, axis=1))
        a_high = narrow[: 2 * L, :]
        u = dot(a_high, high) + dot(narrow[2 * L :, :], high) + dot(a_high, low)
        v_high, v_low = split(jnp.concatenate([spread(u, n) for n in range(2)], axis=0))
        d_high = wide[: 2 * L, :]
        spectrum[p] = dot(v_high, d_high) + dot(v_low, d_high) + dot(v_high, wide[2 * L : 4 * L, :])
        return carry

    lax.fori_loop(0, PAIRS, filter_spectrum, 0)

    for copy in z_copies:
        copy.wait_recv()
    w_c = first_copies(1, w4_send, w4_recv)
    for copy in w_c:
        copy.start()
    for copy in w_a:
        copy.wait_recv()
    w_b = second_copies(0, w3_send, w3_recv)
    for copy in w_b:
        copy.start()

    def b_copy(p, step):
        rows = pl.ds(pl.multiple_of(at_seg(step) * TILES, TILES), TILES)
        return rcopy(
            conv_out.at[pl.ds(2 * p, 2), rows, :],
            conv_in.at[pl.ds(seg * OWN + 2 * p, 2)],
            b_send.at[3 * p + step - 1],
            b_recv.at[3 * p + step - 1],
            (at_seg(step), ch),
        )

    def convolve(p):
        u = dot(narrow[: 2 * L, :], jnp.concatenate([x_in[2 * p], x_in[2 * p + 1]], axis=1))
        v = jnp.concatenate([spread(u, n) for n in range(2)], axis=0)
        x = dot(v.astype(bf16), wide[: 2 * L, :])
        h = spectrum[p]
        x_re, x_im, h_re, h_im = x[:, :L], x[:, L:], h[:, :L], h[:, L:]
        z = jnp.concatenate([x_re * h_re - x_im * h_im, x_re * h_im + x_im * h_re], axis=1)
        e = dot(z.astype(bf16), wide[4 * L : 6 * L, :])
        columns = []
        for n in range(2):
            e_re, e_im = e[n * L : (n + 1) * L, :L], e[n * L : (n + 1) * L, L:]
            re, im = b_re[...], b_im[...]
            columns.append(jnp.concatenate([e_re * re + e_im * im, e_im * re - e_re * im], axis=0))
        y = dot(wide[6 * L :, :], jnp.concatenate(columns, axis=1).astype(bf16)).astype(bf16)
        conv_out[2 * p] = y[:, :L]
        conv_out[2 * p + 1] = y[:, L:]

    for p in range(PAIRS):
        for step in range(1, SEGS):
            x_copy(p, step).wait_recv()
        convolve(p)
        for step in FAR_FIRST:
            b_copy(p, step).start()
    for copy in w_c:
        copy.wait_recv()
    w_d = second_copies(1, w5_send, w5_recv)
    for copy in w_d:
        copy.start()
    conv_in[pl.ds(seg * OWN, OWN)] = conv_out[:, seg_rows, :]

    loads[7].wait()
    loads[8].wait()
    for c in range(HERE):
        skip_v[c : c + 1, :] = jnp.full((1, L), skip_s[c], f32)

    for p in range(PAIRS):
        for step in range(1, SEGS):
            b_copy(p, step).wait_recv()
    for c in range(HERE):
        strip[c * PITCH : c * PITCH + TILES, :] = conv_in[c].astype(f32)

    def gate_tile(j):
        cols = pl.ds(pl.multiple_of(j * L, L), L)
        mixed = key_v[:, cols].astype(f32) * value_v[:, cols].astype(f32)
        conv = strip[pl.ds(j, HERE, stride=PITCH), :]
        return (gate_v[:, cols].astype(f32) * (conv + skip_v[...] * mixed)).astype(bf16)

    gathered[:HERE, :] = gate_tile(chip)
    to_x = [lax.rem(cx + d, NX) * (NY * NZ) for d in range(NX)]
    to_y = [lax.rem(cy + d, NY) * NZ for d in range(NY)]
    to_z = [cz, 1 - cz]
    hops = sorted(
        ((dx, dy, dz) for dx in range(NX) for dy in range(NY) for dz in range(NZ) if dx or dy or dz),
        key=lambda d: -(min(d[0], NX - d[0]) + min(d[1], NY - d[1]) + d[2]),
    )
    sends = []
    for n, (dx, dy, dz) in enumerate(hops):
        target = to_x[dx] + to_y[dy] + to_z[dz]
        slot = (dz * NY + (NY - dy) % NY) * NX + (NX - dx) % NX
        outgoing[n] = gate_tile(target)
        sends.append(
            rcopy(
                outgoing.at[n], gathered.at[slot * HERE : (slot + 1) * HERE, :], g_send, g_recv, at_chip(target)
            )
        )
        if n:
            sends[n - 1].start()
    sends[-1].start()

    def wait_bytes(ref, sem):
        pltpu.make_async_copy(ref, ref, sem).wait()

    for copy in w_b + w_d:
        copy.wait_recv()
    others = pl.ds(HERE, (CHIPS - 1) * HERE)
    wait_bytes(gathered.at[others, :], g_recv)

    def p_copy(n):
        cols = pl.ds(n * COLS, COLS)
        return rcopy(
            partial.at[1 - core, :, cols],
            partner.at[:, cols],
            p_send.at[n],
            p_recv.at[n],
            other_core,
        )

    rows_here = L // CORES
    for n in range(CHUNKS):
        cols = pl.ds(n * COLS, COLS)
        sums = lax.dot_general(
            gathered[...],
            w_all[:, :, :, :, cols].reshape(CHIPS * HERE, COLS),
            (((0,), (0,)), ((), ())),
            preferred_element_type=f32,
        )
        partial[0, :, cols] = sums[:rows_here]
        partial[1, :, cols] = sums[rows_here:]
        if n:
            p_copy(n - 1).start()
    p_copy(CHUNKS - 1).start()
    for n in range(CHUNKS):
        cols = pl.ds(n * COLS, COLS)
        p_copy(n).wait_recv()
        out_ref[:, cols] = (partial[core, :, cols] + partner[:, cols]).astype(bf16)

    for p in range(PAIRS):
        for step in range(1, SEGS):
            x_copy(p, step).wait_send()
            b_copy(p, step).wait_send()
    for copy in z_copies + w_a + w_b + w_c + w_d:
        copy.wait_send()
    wait_bytes(gathered.at[others, :], g_send)
    for n in range(CHUNKS):
        p_copy(n).wait_send()


def on_device(*args):
    anywhere = pl.BlockSpec(memory_space=pltpu.HBM)
    wide, narrow, twiddle = tables()
    dma = pltpu.SemaphoreType.DMA
    return pl.pallas_call(
        kernel,
        out_shape=pltpu.VMEM((L // CORES, D), bf16),
        in_specs=[anywhere] * 9,
        out_specs=pl.BlockSpec(memory_space=pltpu.VMEM),
        scratch_shapes=[
            pltpu.VMEM((HERE, LOCAL), bf16),
            pltpu.VMEM((HERE, LOCAL), bf16),
            pltpu.VMEM((HERE, LOCAL), bf16),
            pltpu.VMEM((WIN, T), f32),
            pltpu.VMEM(wide.shape, bf16),
            pltpu.VMEM(narrow.shape, bf16),
            pltpu.VMEM(twiddle.shape, f32),
            pltpu.SMEM((HERE,), f32),
            pltpu.VMEM((HERE * PITCH, L), f32),
            pltpu.VMEM((HERE, TILES, L), bf16),
            pltpu.VMEM((OWN, T // L, L), bf16),
            pltpu.VMEM((WIN * KPITCH, L), f32),
            pltpu.VMEM((PAIRS, 2 * L, 2 * L), f32),
            pltpu.VMEM((OWN, T // L, L), bf16),
            pltpu.VMEM((HERE, TILES, L), bf16),
            pltpu.VMEM((HERE, L), f32),
            pltpu.VMEM((CHIPS, HERE, L), bf16),
            pltpu.VMEM((CHIPS * HERE, L), bf16),
            pltpu.VMEM((NZ, NY, NX, HERE, D), bf16),
            pltpu.VMEM((CORES, L // CORES, D), f32),
            pltpu.VMEM((L // CORES, D), f32),
            dma((9,)), dma((9,)), dma((9,)), dma((9,)), dma((9,)), dma((2,)), dma((2,)),
            dma((6,)), dma((6,)), dma((6,)), dma((6,)), dma((6,)), dma((6,)), dma((6,)), dma((6,)),
            dma, dma, dma((CHUNKS,)), dma((CHUNKS,)),
        ],
        compiler_params=pltpu.CompilerParams(
            collective_id=0, has_side_effects=True, vmem_limit_bytes=60 * 1024 * 1024
        ),
        name="layer",
    )(*args, jnp.asarray(wide), jnp.asarray(narrow), jnp.asarray(twiddle))


def solution(mesh):
    return jax.shard_map(
        on_device,
        mesh=mesh,
        in_specs=(P("ch", "seg"), P("ch", "seg"), P("ch", "seg"), P("ch", None), P("ch"), P("ch", None)),
        out_specs=P(("seg", "ch"), None),
        check_vma=False,
    )
```

profile of v0, /device:TPU:1, one launch (start us, length us, event | category | flops | bytes accessed | tf_op | source)
XLA Modules:
  0.0 36.1 jit_solution(3926619124034451883)
XLA Ops:
  0.0 35.4 %layer.1 = bf16[64,1536]{1,0:T(8,128)(2,1)S(1)} custom-call(bf16[24,4096]{1,0:T(8,128)(2,1)} %gate_h.1, bf16[24,4096]{1,0:T(8,128)(2,1)} %key_h.1, bf16[24,4096]{1,0:T(8,128)(2,1)} %value_h.1, f32[24,16384]{1,0:T(8,128)} %filt_h.1, f32[24]{0:T(128)} %skip_h.1, bf16[24,1536]{1,0:T(8,128)(2,1)} %weight_h.1, bf16[896,256]{1,0:T(8,128)(2,1)} %constant.6.clone.wide_h, ...), custom_call_target="tpu_custom_call" | custom-call | tf_op jit(solution)/shard_map/layer/pallas_call | solution.py:372
  35.4 0.7 %copy.11 = bf16[64,1536]{1,0:T(8,128)(2,1)} copy(bf16[64,1536]{1,0:T(8,128)(2,1)S(1)} %layer.1) | data formatting | bytes 393216
where the time goes:
time: 36.2 us; the launch traced here: 36.1 us
  Pallas kernels  35.4 us (98%)
  local copies, waits for them, and re-layouts  0.68 us (2%)
    pallas_call x1, Pallas kernels, on_device(): pl.pallas_call(kernel, out_shape=pltpu.VMEM((L // CORES, D), bf16), in_sp...  35.4 us

commit v1 on v0

--- a/solution.py
+++ b/solution.py
@@ -29,6 +29,7 @@
 HALF = D // 2
 PAIRS = OWN // 2
 FAR_FIRST = (2, 1, 3)
+ALL, NEAR = (1, 2, 3), (1, 3)
 
 
 def halves(table):
@@ -94,13 +95,16 @@
     for device in (other_core, across):
         pl.semaphore_signal(barrier, inc=1, device_id=device, device_id_type=MESH)
 
-    def greet(step, carry):
-        pl.semaphore_signal(
-            barrier, inc=1, device_id=at_chip(lax.rem(chip + step, CHIPS)), device_id_type=MESH
-        )
-        return carry
-
-    lax.fori_loop(1, CHIPS, greet, 0)
+    to_x = [lax.rem(cx + d, NX) * (NY * NZ) for d in range(NX)]
+    to_y = [lax.rem(cy + d, NY) * NZ for d in range(NY)]
+    to_z = [cz, 1 - cz]
+    hops = sorted(
+        ((dx, dy, dz) for dx in range(NX) for dy in range(NY) for dz in range(NZ) if dx or dy or dz),
+        key=lambda d: -(min(d[0], NX - d[0]) + min(d[1], NY - d[1]) + d[2]),
+    )
+    targets = [to_x[dx] + to_y[dy] + to_z[dz] for dx, dy, dz in hops]
+    for target in targets:
+        pl.semaphore_signal(barrier, inc=1, device_id=at_chip(target), device_id_type=MESH)
 
     window = pl.multiple_of(lax.div(seg, 2) * 8, 8)
     loads = [
@@ -154,10 +158,20 @@
         )
 
     left, right = pl.ds(0, HALF), pl.ds(HALF, HALF)
-    z_copies = [
-        rcopy(w_all.at[0, 0, 0, :, cols], w_all.at[1, 0, 0, :, cols], w1_send.at[n], w1_recv.at[n], device)
-        for n, (cols, device) in enumerate(((left, at_chip(beside)), (right, across)))
-    ]
+    sides = (at_chip(beside), across)
+
+    def z_pair(there, here, n):
+        return [
+            rcopy(here[m], there[m], w1_send.at[2 * n + m], w1_recv.at[2 * n + m], sides[m]) for m in range(2)
+        ]
+
+    def z_stage(n, *slots):
+        return z_pair([w_all.at[(1, *slot)] for slot in slots], [w_all.at[(0, *slot)] for slot in slots], n)
+
+    every = slice(None)
+    z_copies = z_stage(0, (0, 0, every, left), (0, 0, every, right))
+    z_far = z_stage(1, (0, 2), (2, 0))
+    z_rest = z_stage(2, (2, slice(1, NX), every, left), (slice(1, NY), 2, every, right))
 
     def x_peer(step):
         return at_chip((lax.rem(cx + step, NX) * NY + cy) * NZ + cz)
@@ -165,34 +179,33 @@
     def y_peer(step):
         return at_chip((cx * NY + lax.rem(cy + step, NY)) * NZ + cz)
 
-    def first_copies(z, send, recv):
+    def first_copies(z, steps, send, recv):
         own = w_all.at[z, 0, 0]
         return [
             rcopy(own, w_all.at[z, 0, NX - step], send.at[step - 1], recv.at[step - 1], x_peer(step))
-            for step in range(1, NX)
+            for step in steps
         ] + [
             rcopy(own, w_all.at[z, NY - step, 0], send.at[step + 2], recv.at[step + 2], y_peer(step))
-            for step in range(1, NY)
+            for step in steps
         ]
 
-    def second_copies(z, send, recv):
+    def second_copies(z, steps, send, recv):
         along_x, along_y = w_all.at[z, 0, 1:, :, left], w_all.at[z, 1:, 0, :, right]
         return [
             rcopy(along_x, w_all.at[z, NY - step, 1:, :, left], send.at[step - 1], recv.at[step - 1], y_peer(step))
-            for step in range(1, NY)
+            for step in steps
         ] + [
             rcopy(along_y, w_all.at[z, 1:, NX - step, :, right], send.at[step + 2], recv.at[step + 2], x_peer(step))
-            for step in range(1, NX)
+            for step in steps
         ]
 
     loads[2].wait()
-    w_a = first_copies(0, w2_send, w2_recv)
+    w_a = first_copies(0, ALL, w2_send, w2_recv)
+    for copy in z_copies + w_a:
+        copy.start()
     for p in range(PAIRS):
         for step in FAR_FIRST:
             x_copy(p, step).start()
-        if p == 0:
-            for copy in z_copies + w_a:
-                copy.start()
     x_in[:, seg_rows, :] = mixed_b[pl.ds(seg * OWN, OWN)]
 
     loads[3].wait()
@@ -229,13 +242,13 @@
 
     for copy in z_copies:
         copy.wait_recv()
-    w_c = first_copies(1, w4_send, w4_recv)
+    w_c = first_copies(1, NEAR, w4_send, w4_recv)
     for copy in w_c:
         copy.start()
     for copy in w_a:
         copy.wait_recv()
-    w_b = second_copies(0, w3_send, w3_recv)
-    for copy in w_b:
+    w_b = second_copies(0, ALL, w3_send, w3_recv)
+    for copy in w_b + z_far:
         copy.start()
 
     def b_copy(p, step):
@@ -271,10 +284,14 @@
         convolve(p)
         for step in FAR_FIRST:
             b_copy(p, step).start()
-    for copy in w_c:
+    for copy in w_c + z_far:
         copy.wait_recv()
-    w_d = second_copies(1, w5_send, w5_recv)
+    w_d = second_copies(1, NEAR, w5_send, w5_recv)
     for copy in w_d:
+        copy.start()
+    for copy in w_b:
+        copy.wait_recv()
+    for copy in z_rest:
         copy.start()
     conv_in[pl.ds(seg * OWN, OWN)] = conv_out[:, seg_rows, :]
 
@@ -296,16 +313,9 @@
         return (gate_v[:, cols].astype(f32) * (conv + skip_v[...] * mixed)).astype(bf16)
 
     gathered[:HERE, :] = gate_tile(chip)
-    to_x = [lax.rem(cx + d, NX) * (NY * NZ) for d in range(NX)]
-    to_y = [lax.rem(cy + d, NY) * NZ for d in range(NY)]
-    to_z = [cz, 1 - cz]
-    hops = sorted(
-        ((dx, dy, dz) for dx in range(NX) for dy in range(NY) for dz in range(NZ) if dx or dy or dz),
-        key=lambda d: -(min(d[0], NX - d[0]) + min(d[1], NY - d[1]) + d[2]),
-    )
     sends = []
     for n, (dx, dy, dz) in enumerate(hops):
-        target = to_x[dx] + to_y[dy] + to_z[dz]
+        target = targets[n]
         slot = (dz * NY + (NY - dy) % NY) * NX + (NX - dx) % NX
         outgoing[n] = gate_tile(target)
         sends.append(
@@ -320,7 +330,7 @@
     def wait_bytes(ref, sem):
         pltpu.make_async_copy(ref, ref, sem).wait()
 
-    for copy in w_b + w_d:
+    for copy in w_d + z_rest:
         copy.wait_recv()
     others = pl.ds(HERE, (CHIPS - 1) * HERE)
     wait_bytes(gathered.at[others, :], g_recv)
@@ -358,7 +368,7 @@
         for step in range(1, SEGS):
             x_copy(p, step).wait_send()
             b_copy(p, step).wait_send()
-    for copy in z_copies + w_a + w_b + w_c + w_d:
+    for copy in z_copies + z_far + z_rest + w_a + w_b + w_c + w_d:
         copy.wait_send()
     wait_bytes(gathered.at[others, :], g_send)
     for n in range(CHUNKS):
@@ -396,7 +406,7 @@
             pltpu.VMEM((NZ, NY, NX, HERE, D), bf16),
             pltpu.VMEM((CORES, L // CORES, D), f32),
             pltpu.VMEM((L // CORES, D), f32),
-            dma((9,)), dma((9,)), dma((9,)), dma((9,)), dma((9,)), dma((2,)), dma((2,)),
+            dma((9,)), dma((9,)), dma((9,)), dma((9,)), dma((9,)), dma((6,)), dma((6,)),
             dma((6,)), dma((6,)), dma((6,)), dma((6,)), dma((6,)), dma((6,)), dma((6,)), dma((6,)),
             dma, dma, dma((CHUNKS,)), dma((CHUNKS,)),
         ],

time: 36.2 us -> 34.9 us (0.964)
  Pallas kernels: 35.4 us -> 34.1 us
    pallas_call x1, Pallas kernels: 35.4 us -> 34.1 us  [on_device(): pl.pallas_call(kernel, out_shape=pltpu.VMEM((L // CORES, D), bf16), in_sp...]
where the time goes in v1:
time: 34.9 us; the launch traced here: 34.8 us
  Pallas kernels  34.1 us (98%)
  local copies, waits for them, and re-layouts  0.68 us (2%)
    pallas_call x1, Pallas kernels, on_device(): pl.pallas_call(kernel, out_shape=pltpu.VMEM((L // CORES, D), bf16), in_sp...  34.1 us

profile of v1, /device:TPU:1, one launch (start us, length us, event | category | flops | bytes accessed | tf_op | source)
XLA Modules:
  0.0 34.8 jit_solution(3317126036513049409)
XLA Ops:
  0.0 34.1 %layer.1 = bf16[64,1536]{1,0:T(8,128)(2,1)S(1)} custom-call(bf16[24,4096]{1,0:T(8,128)(2,1)} %gate_h.1, bf16[24,4096]{1,0:T(8,128)(2,1)} %key_h.1, bf16[24,4096]{1,0:T(8,128)(2,1)} %value_h.1, f32[24,16384]{1,0:T(8,128)} %filt_h.1, f32[24]{0:T(128)} %skip_h.1, bf16[24,1536]{1,0:T(8,128)(2,1)} %weight_h.1, bf16[896,256]{1,0:T(8,128)(2,1)} %constant.6.clone.wide_h, ...), custom_call_target="tpu_custom_call" | custom-call | tf_op jit(solution)/shard_map/layer/pallas_call | solution.py:382
  34.2 0.7 %copy.11 = bf16[64,1536]{1,0:T(8,128)(2,1)} copy(bf16[64,1536]{1,0:T(8,128)(2,1)S(1)} %layer.1) | data formatting | bytes 393216

commit v2 on v1

--- a/solution.py
+++ b/solution.py
@@ -24,7 +24,7 @@
 PITCH = TILES + 8
 KPITCH = T // L + 8
 WIN = 16
-CHUNKS = 4
+CHUNKS = 2
 COLS = D // CHUNKS
 HALF = D // 2
 PAIRS = OWN // 2
@@ -103,8 +103,9 @@
         key=lambda d: -(min(d[0], NX - d[0]) + min(d[1], NY - d[1]) + d[2]),
     )
     targets = [to_x[dx] + to_y[dy] + to_z[dz] for dx, dy, dz in hops]
-    for target in targets:
-        pl.semaphore_signal(barrier, inc=1, device_id=at_chip(target), device_id_type=MESH)
+    for (dx, dy, dz), target in zip(hops, targets):
+        if (dx > 0) + (dy > 0) + (dz > 0) == 1:
+            pl.semaphore_signal(barrier, inc=1, device_id=at_chip(target), device_id_type=MESH)
 
     window = pl.multiple_of(lax.div(seg, 2) * 8, 8)
     loads = [
@@ -144,7 +145,7 @@
     for c in range(HERE):
         mixed_b[c] = strip[c * PITCH : c * PITCH + TILES, :].astype(bf16)
 
-    pl.semaphore_wait(barrier, SEGS - 1 + 2 + CHIPS - 1)
+    pl.semaphore_wait(barrier, SEGS - 1 + 2 + NX - 1 + NY - 1 + NZ - 1)
 
     seg_rows = pl.ds(pl.multiple_of(seg * TILES, TILES), TILES)
 
@@ -289,10 +290,6 @@
     w_d = second_copies(1, NEAR, w5_send, w5_recv)
     for copy in w_d:
         copy.start()
-    for copy in w_b:
-        copy.wait_recv()
-    for copy in z_rest:
-        copy.start()
     conv_in[pl.ds(seg * OWN, OWN)] = conv_out[:, seg_rows, :]
 
     loads[7].wait()
@@ -327,6 +324,11 @@
             sends[n - 1].start()
     sends[-1].start()
 
+    for copy in w_b:
+        copy.wait_recv()
+    for copy in z_rest:
+        copy.start()
+
     def wait_bytes(ref, sem):
         pltpu.make_async_copy(ref, ref, sem).wait()
 
@@ -346,12 +348,13 @@
         )
 
     rows_here = L // CORES
+    turned = gathered[...].T
     for n in range(CHUNKS):
         cols = pl.ds(n * COLS, COLS)
         sums = lax.dot_general(
-            gathered[...],
+            turned,
             w_all[:, :, :, :, cols].reshape(CHIPS * HERE, COLS),
-            (((0,), (0,)), ((), ())),
+            (((1,), (0,)), ((), ())),
             preferred_element_type=f32,
         )
         partial[0, :, cols] = sums[:rows_here]

time: 34.9 us -> 34.2 us (0.980)
  Pallas kernels: 34.1 us -> 33.4 us
    pallas_call x1, Pallas kernels: 34.1 us -> 33.4 us  [on_device(): pl.pallas_call(kernel, out_shape=pltpu.VMEM((L // CORES, D), bf16), in_sp...]
where the time goes in v2:
time: 34.2 us; the launch traced here: 34.1 us
  Pallas kernels  33.4 us (98%)
  local copies, waits for them, and re-layouts  0.68 us (2%)
    pallas_call x1, Pallas kernels, on_device(): pl.pallas_call(kernel, out_shape=pltpu.VMEM((L // CORES, D), bf16), in_sp...  33.4 us

profile of v2, /device:TPU:1, one launch (start us, length us, event | category | flops | bytes accessed | tf_op | source)
XLA Modules:
  0.0 34.1 jit_solution(140762117276165953)
XLA Ops:
  0.0 33.4 %layer.1 = bf16[64,1536]{1,0:T(8,128)(2,1)S(1)} custom-call(bf16[24,4096]{1,0:T(8,128)(2,1)} %gate_h.1, bf16[24,4096]{1,0:T(8,128)(2,1)} %key_h.1, bf16[24,4096]{1,0:T(8,128)(2,1)} %value_h.1, f32[24,16384]{1,0:T(8,128)} %filt_h.1, f32[24]{0:T(128)} %skip_h.1, bf16[24,1536]{1,0:T(8,128)(2,1)} %weight_h.1, bf16[896,256]{1,0:T(8,128)(2,1)} %constant.6.clone.wide_h, ...), custom_call_target="tpu_custom_call" | custom-call | tf_op jit(solution)/shard_map/layer/pallas_call | solution.py:385
  33.4 0.7 %copy.11 = bf16[64,1536]{1,0:T(8,128)(2,1)} copy(bf16[64,1536]{1,0:T(8,128)(2,1)S(1)} %layer.1) | data formatting | bytes 393216

commit v3 on v2

--- a/solution.py
+++ b/solution.py
@@ -69,7 +69,7 @@
     out_ref,
     gate_v, key_v, value_v, filt_v, wide, narrow, twiddle,
     skip_s, strip, mixed_b, x_in, filt_x, spectrum, conv_out, conv_in, skip_v,
-    outgoing, gathered, w_all, partial, partner,
+    outgoing, gathered, w_all, partial, leaving, partner,
     load_sem, x_send, x_recv, b_send, b_recv, w1_send, w1_recv,
     w2_send, w2_recv, w3_send, w3_recv, w4_send, w4_recv, w5_send, w5_recv,
     g_send, g_recv, p_send, p_recv,
@@ -204,9 +204,17 @@
     w_a = first_copies(0, ALL, w2_send, w2_recv)
     for copy in z_copies + w_a:
         copy.start()
-    for p in range(PAIRS):
-        for step in FAR_FIRST:
-            x_copy(p, step).start()
+    def x_start(*pairs):
+        for p in pairs:
+            for step in FAR_FIRST:
+                x_copy(p, step).start()
+
+    x_start(0)
+
+    @pl.when(core == 0)
+    def _():
+        x_start(1, 2)
+
     x_in[:, seg_rows, :] = mixed_b[pl.ds(seg * OWN, OWN)]
 
     loads[3].wait()
@@ -240,6 +248,10 @@
         return carry
 
     lax.fori_loop(0, PAIRS, filter_spectrum, 0)
+
+    @pl.when(core == 1)
+    def _():
+        x_start(1, 2)
 
     for copy in z_copies:
         copy.wait_recv()
@@ -340,7 +352,7 @@
     def p_copy(n):
         cols = pl.ds(n * COLS, COLS)
         return rcopy(
-            partial.at[1 - core, :, cols],
+            leaving.at[1 - core, :, cols],
             partner.at[:, cols],
             p_send.at[n],
             p_recv.at[n],
@@ -359,13 +371,15 @@
         )
         partial[0, :, cols] = sums[:rows_here]
         partial[1, :, cols] = sums[rows_here:]
+        leaving[0, :, cols] = sums[:rows_here].astype(bf16)
+        leaving[1, :, cols] = sums[rows_here:].astype(bf16)
         if n:
             p_copy(n - 1).start()
     p_copy(CHUNKS - 1).start()
     for n in range(CHUNKS):
         cols = pl.ds(n * COLS, COLS)
         p_copy(n).wait_recv()
-        out_ref[:, cols] = (partial[core, :, cols] + partner[:, cols]).astype(bf16)
+        out_ref[:, cols] = (partial[core, :, cols] + partner[:, cols].astype(f32)).astype(bf16)
 
     for p in range(PAIRS):
         for step in range(1, SEGS):
@@ -408,7 +422,8 @@
             pltpu.VMEM((CHIPS * HERE, L), bf16),
             pltpu.VMEM((NZ, NY, NX, HERE, D), bf16),
             pltpu.VMEM((CORES, L // CORES, D), f32),
-            pltpu.VMEM((L // CORES, D), f32),
+            pltpu.VMEM((CORES, L // CORES, D), bf16),
+            pltpu.VMEM((L // CORES, D), bf16),
             dma((9,)), dma((9,)), dma((9,)), dma((9,)), dma((9,)), dma((6,)), dma((6,)),
             dma((6,)), dma((6,)), dma((6,)), dma((6,)), dma((6,)), dma((6,)), dma((6,)), dma((6,)),
             dma, dma, dma((CHUNKS,)), dma((CHUNKS,)),

time: 34.2 us -> 33.6 us (0.982)
  Pallas kernels: 33.4 us -> 32.8 us
    pallas_call x1, Pallas kernels: 33.4 us -> 32.8 us  [on_device(): pl.pallas_call(kernel, out_shape=pltpu.VMEM((L // CORES, D), bf16), in_sp...]
where the time goes in v3:
time: 33.6 us; the launch traced here: 33.5 us
  Pallas kernels  32.8 us (98%)
  local copies, waits for them, and re-layouts  0.68 us (2%)
    pallas_call x1, Pallas kernels, on_device(): pl.pallas_call(kernel, out_shape=pltpu.VMEM((L // CORES, D), bf16), in_sp...  32.8 us
    unnamed x1, local copies, waits for them, and re-layouts  0.68 us

profile of v3, /device:TPU:1, one launch (start us, length us, event | category | flops | bytes accessed | tf_op | source)
XLA Modules:
  0.0 33.5 jit_solution(3540765015676911221)
XLA Ops:
  0.0 32.8 %layer.1 = bf16[64,1536]{1,0:T(8,128)(2,1)S(1)} custom-call(bf16[24,4096]{1,0:T(8,128)(2,1)} %gate_h.1, bf16[24,4096]{1,0:T(8,128)(2,1)} %key_h.1, bf16[24,4096]{1,0:T(8,128)(2,1)} %value_h.1, f32[24,16384]{1,0:T(8,128)} %filt_h.1, f32[24]{0:T(128)} %skip_h.1, bf16[24,1536]{1,0:T(8,128)(2,1)} %weight_h.1, bf16[896,256]{1,0:T(8,128)(2,1)} %constant.6.clone.wide_h, ...), custom_call_target="tpu_custom_call" | custom-call | tf_op jit(solution)/shard_map/layer/pallas_call | solution.py:399
  32.8 0.7 %copy.11 = bf16[64,1536]{1,0:T(8,128)(2,1)} copy(bf16[64,1536]{1,0:T(8,128)(2,1)S(1)} %layer.1) | data formatting | bytes 393216

commit v4 on v3

--- a/solution.py
+++ b/solution.py
@@ -209,10 +209,9 @@
             for step in FAR_FIRST:
                 x_copy(p, step).start()
 
-    x_start(0)
-
     @pl.when(core == 0)
     def _():
+        x_start(0)
         x_start(1, 2)
 
     x_in[:, seg_rows, :] = mixed_b[pl.ds(seg * OWN, OWN)]
@@ -226,6 +225,10 @@
         return carry
 
     lax.fori_loop(0, T // L, turn, 0, unroll=4)
+
+    @pl.when(core == 1)
+    def _():
+        x_start(0)
 
     first = seg * OWN - window
     b_re, b_im = twiddle.at[:L, :], twiddle.at[L:, :]
@@ -275,21 +278,21 @@
         )
 
     def convolve(p):
-        u = dot(narrow[: 2 * L, :], jnp.concatenate([x_in[2 * p], x_in[2 * p + 1]], axis=1))
-        v = jnp.concatenate([spread(u, n) for n in range(2)], axis=0)
-        x = dot(v.astype(bf16), wide[: 2 * L, :])
-        h = spectrum[p]
-        x_re, x_im, h_re, h_im = x[:, :L], x[:, L:], h[:, :L], h[:, L:]
-        z = jnp.concatenate([x_re * h_re - x_im * h_im, x_re * h_im + x_im * h_re], axis=1)
-        e = dot(z.astype(bf16), wide[4 * L : 6 * L, :])
-        columns = []
-        for n in range(2):
-            e_re, e_im = e[n * L : (n + 1) * L, :L], e[n * L : (n + 1) * L, L:]
-            re, im = b_re[...], b_im[...]
-            columns.append(jnp.concatenate([e_re * re + e_im * im, e_im * re - e_re * im], axis=0))
-        y = dot(wide[6 * L :, :], jnp.concatenate(columns, axis=1).astype(bf16)).astype(bf16)
-        conv_out[2 * p] = y[:, :L]
-        conv_out[2 * p + 1] = y[:, L:]
+        pair = range(2)
+        us = [dot(narrow[: 2 * L, :], x_in[2 * p + n]) for n in pair]
+        xs = [dot(spread(u, 0).astype(bf16), wide[: 2 * L, :]) for u in us]
+        zs = []
+        for n in pair:
+            h, x = spectrum[p, n * L : (n + 1) * L, :], xs[n]
+            x_re, x_im, h_re, h_im = x[:, :L], x[:, L:], h[:, :L], h[:, L:]
+            zs.append(jnp.concatenate([x_re * h_re - x_im * h_im, x_re * h_im + x_im * h_re], axis=1))
+        es = [dot(z.astype(bf16), wide[4 * L : 6 * L, :]) for z in zs]
+        fs = []
+        for e in es:
+            e_re, e_im, re, im = e[:, :L], e[:, L:], b_re[...], b_im[...]
+            fs.append(jnp.concatenate([e_re * re + e_im * im, e_im * re - e_re * im], axis=0).astype(bf16))
+        for n in pair:
+            conv_out[2 * p + n] = dot(wide[6 * L :, :], fs[n]).astype(bf16)
 
     for p in range(PAIRS):
         for step in range(1, SEGS):
@@ -312,8 +315,9 @@
     for p in range(PAIRS):
         for step in range(1, SEGS):
             b_copy(p, step).wait_recv()
-    for c in range(HERE):
-        strip[c * PITCH : c * PITCH + TILES, :] = conv_in[c].astype(f32)
+        for c in range(HERE):
+            if c % OWN // 2 == p:
+                strip[c * PITCH : c * PITCH + TILES, :] = conv_in[c].astype(f32)
 
     def gate_tile(j):
         cols = pl.ds(pl.multiple_of(j * L, L), L)

time: 33.6 us -> 33.3 us (level)
  no operation moved by 1% of the time
where the time goes in v4:
time: 33.3 us; the launch traced here: 33.2 us
  Pallas kernels  32.5 us (98%)
  local copies, waits for them, and re-layouts  0.68 us (2%)
    pallas_call x1, Pallas kernels, on_device(): pl.pallas_call(kernel, out_shape=pltpu.VMEM((L // CORES, D), bf16), in_sp...  32.5 us
    unnamed x1, local copies, waits for them, and re-layouts  0.68 us

profile of v4, /device:TPU:1, one launch (start us, length us, event | category | flops | bytes accessed | tf_op | source)
XLA Modules:
  0.0 33.2 jit_solution(4996965196855151066)
XLA Ops:
  0.0 32.5 %layer.1 = bf16[64,1536]{1,0:T(8,128)(2,1)S(1)} custom-call(bf16[24,4096]{1,0:T(8,128)(2,1)} %gate_h.1, bf16[24,4096]{1,0:T(8,128)(2,1)} %key_h.1, bf16[24,4096]{1,0:T(8,128)(2,1)} %value_h.1, f32[24,16384]{1,0:T(8,128)} %filt_h.1, f32[24]{0:T(128)} %skip_h.1, bf16[24,1536]{1,0:T(8,128)(2,1)} %weight_h.1, bf16[896,256]{1,0:T(8,128)(2,1)} %constant.6.clone.wide_h, ...), custom_call_target="tpu_custom_call" | custom-call | tf_op jit(solution)/shard_map/layer/pallas_call | solution.py:403
  32.5 0.7 %copy.11 = bf16[64,1536]{1,0:T(8,128)(2,1)} copy(bf16[64,1536]{1,0:T(8,128)(2,1)S(1)} %layer.1) | data formatting | bytes 393216

commit v5 on v4

--- a/solution.py
+++ b/solution.py
@@ -202,7 +202,7 @@
 
     loads[2].wait()
     w_a = first_copies(0, ALL, w2_send, w2_recv)
-    for copy in z_copies + w_a:
+    for copy in z_copies:
         copy.start()
     def x_start(*pairs):
         for p in pairs:
@@ -214,6 +214,8 @@
         x_start(0)
         x_start(1, 2)
 
+    for copy in w_a:
+        copy.start()
     x_in[:, seg_rows, :] = mixed_b[pl.ds(seg * OWN, OWN)]
 
     loads[3].wait()

time: 33.3 us -> 33.3 us (level)
  no operation moved by 1% of the time
where the time goes in v5:
time: 33.3 us; the launch traced here: 33.2 us
  Pallas kernels  32.5 us (98%)
  local copies, waits for them, and re-layouts  0.68 us (2%)
    pallas_call x1, Pallas kernels, on_device(): pl.pallas_call(kernel, out_shape=pltpu.VMEM((L // CORES, D), bf16), in_sp...  32.5 us
    unnamed x1, local copies, waits for them, and re-layouts  0.68 us

profile of v5, /device:TPU:1, one launch (start us, length us, event | category | flops | bytes accessed | tf_op | source)
XLA Modules:
  0.0 33.2 jit_solution(3058132174477755401)
XLA Ops:
  0.0 32.5 %layer.1 = bf16[64,1536]{1,0:T(8,128)(2,1)S(1)} custom-call(bf16[24,4096]{1,0:T(8,128)(2,1)} %gate_h.1, bf16[24,4096]{1,0:T(8,128)(2,1)} %key_h.1, bf16[24,4096]{1,0:T(8,128)(2,1)} %value_h.1, f32[24,16384]{1,0:T(8,128)} %filt_h.1, f32[24]{0:T(128)} %skip_h.1, bf16[24,1536]{1,0:T(8,128)(2,1)} %weight_h.1, bf16[896,256]{1,0:T(8,128)(2,1)} %constant.6.clone.wide_h, ...), custom_call_target="tpu_custom_call" | custom-call | tf_op jit(solution)/shard_map/layer/pallas_call | solution.py:405
  32.5 0.7 %copy.11 = bf16[64,1536]{1,0:T(8,128)(2,1)} copy(bf16[64,1536]{1,0:T(8,128)(2,1)S(1)} %layer.1) | data formatting | bytes 393216

commit v6 on v4

--- a/solution.py
+++ b/solution.py
@@ -254,13 +254,17 @@
 
     @pl.when(core == 1)
     def _():
-        x_start(1, 2)
+        x_start(1)
 
     for copy in z_copies:
         copy.wait_recv()
     w_c = first_copies(1, NEAR, w4_send, w4_recv)
     for copy in w_c:
         copy.start()
+    @pl.when(core == 1)
+    def _():
+        x_start(2)
+
     for copy in w_a:
         copy.wait_recv()
     w_b = second_copies(0, ALL, w3_send, w3_recv)

time: 33.3 us -> 33.4 us (level)
  no operation moved by 1% of the time
where the time goes in v6:
time: 33.4 us; the launch traced here: 33.3 us
  Pallas kernels  32.6 us (98%)
  local copies, waits for them, and re-layouts  0.68 us (2%)
    pallas_call x1, Pallas kernels, on_device(): pl.pallas_call(kernel, out_shape=pltpu.VMEM((L // CORES, D), bf16), in_sp...  32.6 us
    unnamed x1, local copies, waits for them, and re-layouts  0.68 us

profile of v6, /device:TPU:1, one launch (start us, length us, event | category | flops | bytes accessed | tf_op | source)
XLA Modules:
  0.0 33.3 jit_solution(8602947608287174138)
XLA Ops:
  0.0 32.6 %layer.1 = bf16[64,1536]{1,0:T(8,128)(2,1)S(1)} custom-call(bf16[24,4096]{1,0:T(8,128)(2,1)} %gate_h.1, bf16[24,4096]{1,0:T(8,128)(2,1)} %key_h.1, bf16[24,4096]{1,0:T(8,128)(2,1)} %value_h.1, f32[24,16384]{1,0:T(8,128)} %filt_h.1, f32[24]{0:T(128)} %skip_h.1, bf16[24,1536]{1,0:T(8,128)(2,1)} %weight_h.1, bf16[896,256]{1,0:T(8,128)(2,1)} %constant.6.clone.wide_h, ...), custom_call_target="tpu_custom_call" | custom-call | tf_op jit(solution)/shard_map/layer/pallas_call | solution.py:407
  32.6 0.7 %copy.11 = bf16[64,1536]{1,0:T(8,128)(2,1)} copy(bf16[64,1536]{1,0:T(8,128)(2,1)S(1)} %layer.1) | data formatting | bytes 393216
